TPU v7x, 32 devices: a whole 2x2x4 slice. The times are simulated.
32 devices in a mesh: groups: 2 (over y), expert: 16 (over z, x, core).
Axes of the slice: x: 2, y: 2, z: 4, core: 2. Of those that a mesh axis runs over, the one named last changes fastest.
Arguments:
- tokens: bfloat16 [256, 4096], P(('groups', 'expert')), parts along dimension 0, may hold values from -6 to 6
- router: float32 [4096, 8], replicated, may hold values from -0.09375 to 0.09375
- w_gate: bfloat16 [4096, 57344], P(None, 'expert'), may hold values from -0.09375 to 0.09375
- w_up: bfloat16 [4096, 57344], P(None, 'expert'), may hold values from -0.09375 to 0.09375
- w_down: bfloat16 [57344, 4096], P('expert'), may hold values from -0.0625 to 0.0625
- norm_gain: float32 [4096], replicated, may hold values from 0.1 to 1.9
- head_weight: bfloat16 [4096, 16384], P(None, 'expert'), may hold values from -18 to 18
- expert_ids: int32 [256, 2], P(('groups', 'expert')), parts along dimension 0, may hold values from 0 to 7, all different within a row; in each aligned block of 8 rows (0 to 7, 8 to 15, ...) at most 3 rows name the same one
- targets: int32 [256], P(('groups', 'expert')), parts along dimension 0, may hold values from 0 to 16383
- domains: int32 [256], P(('groups', 'expert')), parts along dimension 0, may hold values from 0 to 31
- bins: int32 [256], P(('groups', 'expert')), parts along dimension 0, may hold values from 0 to 15
Outputs:
- hidden_out: bfloat16 [256, 4096], P(('groups', 'expert')), parts along dimension 0
- token_nll: float32 [256], P(('groups', 'expert')), parts along dimension 0
- domain_table: float32 [3, 64, 16], P(None, ('groups', 'expert')), parts along dimension 1
There are 2 independent parts, one for each index of `groups`. A program takes and returns all parts, laid end to end along the dimension named above; an argument that names none is the same for every part. Nothing has to cross between parts.
Inputs may be any that keep to these rules, and one draw needn't show every extreme that they name: `expert_ids`: each token names two different experts. Among the 8 rows of one index of expert, no expert is named more than 3 times, and in some of these blocks one expert is named exactly 3 times.
All inputs are finite; a program needn't handle non-finite values.
Results may differ from a plain program's by a relative error of at most 0.0095.
Values may be sent and summed in bfloat16 or wider, within the bound.
A program may use at most 192 MiB of HBM per device.

v0:
```python
import jax
import jax.numpy as jnp
from jax import lax
from jax.sharding import PartitionSpec as P

EXPERTS = 8
DOM_DEV = 2
BINS = 16
CAP = 3


def joined(value, axis, join):
    pieces = jax.tree.map(lambda part: lax.all_gather(part, axis), value)
    head = jax.tree.map(lambda part: part[0], pieces)
    tail = jax.tree.map(lambda part: part[1:], pieces)
    so_far, _ = lax.scan(lambda so_far, slab: (join(so_far, slab), None), head, tail)
    return so_far


def join_parts(left_part, right_part):
    left_top, left_mass, left_moment, left_target = left_part
    right_top, right_mass, right_moment, right_target = right_part
    joined_top = jnp.maximum(left_top, right_top)
    left_factor = jnp.exp(left_top - joined_top)
    right_factor = jnp.exp(right_top - joined_top)
    return (
        joined_top,
        left_mass * left_factor + right_mass * right_factor,
        left_moment * left_factor + right_moment * right_factor,
        left_target + right_target,
    )


def domain_sums_of(dom_ids, bin_ids, nll_values, ent_values, dom_first, dom_count):
    dom_hot = (
        dom_ids[None, :] == dom_first + jnp.arange(dom_count, dtype=jnp.int32)[:, None]
    ).astype(jnp.float32)
    bin_hot = (bin_ids[:, None] == jnp.arange(BINS, dtype=jnp.int32)[None, :]).astype(jnp.float32)
    columns = jnp.stack([jnp.ones_like(nll_values), nll_values, ent_values], axis=1)
    spread_cols = (columns[:, :, None] * bin_hot[:, None, :]).reshape(nll_values.shape[0], 3 * BINS)
    return jnp.dot(dom_hot, spread_cols, precision=lax.Precision.HIGHEST)


def on_device(
    tokens, router, w_gate, w_up, w_down, norm_gain, head_weight, expert_ids, targets, domains, bins
):
    highest = lax.Precision.HIGHEST
    devices = lax.axis_size("expert")
    per_expert = devices // EXPERTS
    own_rows, model_width = tokens.shape
    my_index = lax.axis_index("expert")
    route_logits = jnp.dot(tokens.astype(jnp.float32), router, precision=highest)
    expert_range = jnp.arange(EXPERTS, dtype=jnp.int32)
    onehot = (expert_ids[:, :, None] == expert_range[None, None, :]).astype(jnp.float32)
    chosen = jnp.sum(onehot * route_logits[:, None, :], axis=2)
    gate_weights = jax.nn.sigmoid(chosen - chosen[:, ::-1])
    flat_pairs = onehot.reshape(own_rows * 2, EXPERTS)
    before = jnp.cumsum(flat_pairs, axis=0) - flat_pairs
    slot_index = jnp.sum(before * flat_pairs, axis=1).reshape(own_rows, 2).astype(jnp.int32)
    slot_hot = (slot_index[:, :, None] == jnp.arange(CAP, dtype=jnp.int32)[None, None, :]).astype(
        jnp.float32
    )
    combine_weights = jnp.einsum("tk,tke,tkc->tec", gate_weights, onehot, slot_hot).reshape(
        own_rows, EXPERTS * CAP
    )
    layout = jnp.einsum("tke,tkc->ect", onehot, slot_hot).astype(jnp.bfloat16)
    packed = jnp.einsum("ect,td->ecd", layout, tokens, preferred_element_type=jnp.float32).astype(
        jnp.bfloat16
    )
    outgoing = jnp.broadcast_to(packed[:, None], (EXPERTS, per_expert, CAP, model_width)).reshape(
        devices, CAP, model_width
    )
    received = lax.all_to_all(outgoing, "expert", split_axis=0, concat_axis=0, tiled=True)
    slot_count = received.shape[1]
    flat_rows = received.reshape(devices * slot_count, model_width)
    gate_act = jnp.dot(flat_rows, w_gate, preferred_element_type=jnp.float32)
    up_act = jnp.dot(flat_rows, w_up, preferred_element_type=jnp.float32)
    act = (jax.nn.silu(gate_act) * up_act).astype(jnp.bfloat16)
    partial_out = jnp.dot(act, w_down, preferred_element_type=jnp.float32).astype(jnp.bfloat16)
    returned = lax.all_to_all(
        partial_out.reshape(devices, slot_count, model_width),
        "expert",
        split_axis=0,
        concat_axis=0,
        tiled=True,
    )
    summed = jnp.sum(
        returned.reshape(EXPERTS, per_expert, CAP, model_width), axis=1, dtype=jnp.float32
    )
    moe_out = jnp.dot(
        combine_weights, summed.reshape(EXPERTS * CAP, model_width), precision=highest
    )
    hidden_out = (tokens.astype(jnp.float32) + moe_out).astype(jnp.bfloat16)
    hidden_wide = hidden_out.astype(jnp.float32)
    normed = (
        hidden_wide
        * lax.rsqrt(jnp.mean(hidden_wide * hidden_wide, axis=1, keepdims=True) + 1.0)
        * norm_gain
    ).astype(jnp.bfloat16)
    vocab_cols = head_weight.shape[1]
    vocab_first = my_index * vocab_cols
    all_targets, all_domains, all_bins = (
        lax.all_gather(targets, "expert", axis=0, tiled=True),
        lax.all_gather(domains, "expert", axis=0, tiled=True),
        lax.all_gather(bins, "expert", axis=0, tiled=True),
    )
    scores = jnp.dot(
        lax.all_gather(normed, "expert", axis=0, tiled=True),
        head_weight,
        preferred_element_type=jnp.float32,
    )
    row_top = jnp.max(scores, axis=1)
    exp_scores = jnp.exp(scores - row_top[:, None])
    mass_sum = jnp.sum(exp_scores, axis=1)
    weighted = jnp.sum(exp_scores * scores, axis=1)
    column_ids = vocab_first + jnp.arange(vocab_cols, dtype=jnp.int32)
    target_score = jnp.sum(
        jnp.where(all_targets[:, None] == column_ids[None, :], scores, 0.0), axis=1
    )
    head_parts = jnp.stack([row_top, mass_sum, weighted, target_score])
    own_first = my_index * own_rows
    joined_top, joined_mass, joined_moment, joined_target = joined(
        (head_parts[0], head_parts[1], head_parts[2], head_parts[3]), "expert", join_parts
    )
    log_norm = joined_top + jnp.log(joined_mass)
    nll_all = log_norm - joined_target
    entropy_all = log_norm - joined_moment / joined_mass
    token_nll = lax.dynamic_slice_in_dim(nll_all, own_first, own_rows, 0)
    table = domain_sums_of(all_domains, all_bins, nll_all, entropy_all, my_index * DOM_DEV, DOM_DEV)
    domain_table = table.reshape(DOM_DEV, 3, BINS).transpose(1, 0, 2)
    return (hidden_out, token_nll, domain_table)


def solution(mesh):
    return jax.shard_map(
        on_device,
        mesh=mesh,
        in_specs=(
            P(("groups", "expert"), None),
            P(),
            P(None, "expert"),
            P(None, "expert"),
            P("expert", None),
            P(),
            P(None, "expert"),
            P(("groups", "expert"), None),
            P(("groups", "expert")),
            P(("groups", "expert")),
            P(("groups", "expert")),
        ),
        out_specs=(
            P(("groups", "expert"), None),
            P(("groups", "expert")),
            P(None, ("groups", "expert"), None),
        ),
        check_vma=False,
    )
```

profile of v0, /device:TPU:0, one launch (start us, length us, event | category | flops | bytes accessed | tf_op | source)
XLA Modules:
  0.0 213.1 jit_solution(17530815499781248772)
XLA Ops:
  7.2 0.8 copy.20
  8.7 1.1 convolution_convert_fusion.1
  10.2 21.5 %all_to_all.10 = bf16[16,3,4096]{2,1,0:T(4,128)(2,1)S(1)} all-to-all(bf16[16,3,4096]{2,1,0:T(4,128)(2,1)S(1)} %bitcast.96), channel_id=1, replica_groups=mesh['groups'=2,'expert'=16] {'expert'}, dimensions={0} | all-to-all | bytes 786432 | tf_op jit(solution)/shard_map/all_to_all | solution.py:73
  31.6 0.3 reshape.79
  32.0 11.9 %fusion.52 = f32[48,3584]{1,0:T(8,128)S(1)} fusion(bf16[48,4096]{1,0:T(8,128)(2,1)S(1)} %reshape.79, bf16[4096,3584]{1,0:T(8,128)(2,1)} %param.15), kind=kOutput, calls=%fused_computation.90 | convolution fusion | flops 1409286144 | bytes 30441472 | tf_op jit(solution)/shard_map/dot_general | solution.py:76
  44.0 21.8 %convolution_convert_fusion = bf16[48,4096]{1,0:T(8,128)(2,1)S(1)} fusion(bf16[3584,4096]{1,0:T(8,128)(2,1)} %param.17, bf16[48,4096]{1,0:T(8,128)(2,1)S(1)} %reshape.79, bf16[4096,3584]{1,0:T(8,128)(2,1)} %param.16, f32[48,3584]{1,0:T(8,128)S(1)} %fusion.52), kind=kOutput, calls=%fused_computation.18 | convolution fusion | flops 2819801088 | bytes 60194816 | tf_op jit(solution)/shard_map/dot_general | solution.py:79
  65.8 1.0 reshape.80
  66.9 4.2 %all-to-all-start.1 = ((bf16[16,3,4096]{2,1,0:T(4,128)(2,1)}), bf16[16,3,4096]{2,1,0:T(4,128)(2,1)S(1)}, u32[]{:S(2)}, u32[]{:S(2)}) async-start(bf16[16,3,4096]{2,1,0:T(4,128)(2,1)} %reshape.80), calls=%async_computation.1 | async-start | bytes 1048576 | tf_op jit(solution)/shard_map/all_to_all | solution.py:80
  71.9 13.4 %all-to-all-done.1 = bf16[16,3,4096]{2,1,0:T(4,128)(2,1)S(1)} async-done(((bf16[16,3,4096]{2,1,0:T(4,128)(2,1)}), bf16[16,3,4096]{2,1,0:T(4,128)(2,1)S(1)}, u32[]{:S(2)}, u32[]{:S(2)}) %all-to-all-start.1) | async-done | bytes 393248 | tf_op jit(solution)/shard_map/all_to_all | solution.py:80
  85.3 0.3 convert_reduce_fusion
  85.6 1.2 fusion.22
  86.8 0.7 fusion.24
  87.6 0.6 dynamic-slice
  89.5 10.5 %all-reduce.3 = (s32[128]{0:T(128)S(1)}, s32[128]{0:T(128)S(1)}, s32[128]{0:T(128)S(1)}) all-reduce(s32[128]{0:T(128)S(1)} %dynamic-update-slice, s32[128]{0:T(128)S(1)} %dynamic-update-slice.2, s32[128]{0:T(128)S(1)} %dynamic-update-slice.1), channel_id=1, replica_groups=mesh['groups'=2,'expert'=16] {'expert'}, use_global_device_ids=true, to_apply=%add | all-reduce | flops 384 | bytes 3072
  100.1 25.0 %all-gather.10.cloned.1.call-done = bf16[128,4096]{1,0:T(8,128)(2,1)} async-done(((bf16[8,4096]{1,0:T(8,128)(2,1)}), bf16[128,4096]{1,0:T(8,128)(2,1)}) %all-gather.10.cloned.1.call-update) | async-done | bytes 1048592 | tf_op jit(solution)/shard_map/all_gather | solution.py:108
  125.1 5.1 %fusion.50 = (f32[128]{0:T(128)S(1)}, f32[128,1024]{1,0:T(8,128)S(1)}) fusion(bf16[128,4096]{1,0:T(8,128)(2,1)} %all-gather.10.cloned.1.call-done, bf16[4096,1024]{1,0:T(8,128)(2,1)} %param.19), kind=kOutput, calls=%fused_computation.88 | convolution fusion | flops 1073872768 | bytes 9961984 | tf_op jit(solution)/shard_map/dot_general | solution.py:107
  130.2 0.3 multiply_reduce_fusion
  130.5 19.4 %all-gather.7 = f32[16,1,128]{2,1,0:T(1,128)S(1)} all-gather(f32[1,1,128]{2,1,0:T(1,128)S(1)} %bitcast.104), channel_id=5, replica_groups=mesh['groups'=2,'expert'=16] {'expert'}, dimensions={0}, use_global_device_ids=true | all-gather | bytes 8704 | tf_op jit(solution)/shard_map/all_gather | solution.py:13
  149.9 17.4 %all-gather.6 = f32[16,1,128]{2,1,0:T(1,128)S(1)} all-gather(f32[1,1,128]{2,1,0:T(1,128)S(1)} %bitcast.103), channel_id=4, replica_groups=mesh['groups'=2,'expert'=16] {'expert'}, dimensions={0}, use_global_device_ids=true | all-gather | bytes 8704 | tf_op jit(solution)/shard_map/all_gather | solution.py:13
  167.3 18.8 %all-gather.5 = f32[16,1,128]{2,1,0:T(1,128)S(1)} all-gather(f32[1,1,128]{2,1,0:T(1,128)S(1)} %bitcast.102), channel_id=3, replica_groups=mesh['groups'=2,'expert'=16] {'expert'}, dimensions={0}, use_global_device_ids=true | all-gather | bytes 8704 | tf_op jit(solution)/shard_map/all_gather | solution.py:13
  186.1 17.4 %all-gather.4 = f32[16,1,128]{2,1,0:T(1,128)S(1)} all-gather(f32[1,1,128]{2,1,0:T(1,128)S(1)} %bitcast.101), channel_id=2, replica_groups=mesh['groups'=2,'expert'=16] {'expert'}, dimensions={0}, use_global_device_ids=true | all-gather | bytes 8704 | tf_op jit(solution)/shard_map/all_gather | solution.py:13
  203.5 1.2 while.16
  204.8 0.6 dynamic_slice.16
  205.4 0.8 convolution_bitcast_fusion.1
  (102 shorter events, 3.7 us)
Async XLA Ops:
  7.2 63.9 %copy-start = (f32[4096,8]{0,1:T(8,128)S(1)}, f32[4096,8]{0,1:T(8,128)}, u32[]{:S(2)}) copy-start(f32[4096,8]{0,1:T(8,128)} %param.14) | copy-start | bytes 393220
  43.9 27.2 %copy-start.1 = (bf16[8,4096]{1,0:T(8,128)(2,1)S(1)}, bf16[8,4096]{1,0:T(8,128)(2,1)}, u32[]{:S(2)}) copy-start(bf16[8,4096]{1,0:T(8,128)(2,1)} %param.13) | copy-start | bytes 196612
  43.9 42.9 %copy-start.3 = (f32[4096]{0:T(1024)S(1)}, f32[4096]{0:T(1024)}, u32[]{:S(2)}) copy-start(f32[4096]{0:T(1024)} %param.18) | copy-start | bytes 49156
  44.0 43.6 %copy-start.7 = (u32[32]{0:T(128)S(1)}, u32[32]{0:T(128)}, u32[]{:S(2)}) copy-start(u32[32]{0:T(128)} %constant.50) | copy-start | bytes 388
  44.0 44.9 %copy-start.4 = (s32[8]{0:T(128)S(1)}, s32[8]{0:T(128)}, u32[]{:S(2)}) copy-start(s32[8]{0:T(128)} %param.21) | copy-start | bytes 100
  44.0 45.1 %copy-start.5 = (s32[8]{0:T(128)S(1)}, s32[8]{0:T(128)}, u32[]{:S(2)}) copy-start(s32[8]{0:T(128)} %param.22) | copy-start | bytes 100
  44.0 45.3 %copy-start.6 = (s32[8]{0:T(128)S(1)}, s32[8]{0:T(128)}, u32[]{:S(2)}) copy-start(s32[8]{0:T(128)} %param.23) | copy-start | bytes 100
  66.9 18.4 %all-to-all-start.1 = ((bf16[16,3,4096]{2,1,0:T(4,128)(2,1)}), bf16[16,3,4096]{2,1,0:T(4,128)(2,1)S(1)}, u32[]{:S(2)}, u32[]{:S(2)}) async-start(bf16[16,3,4096]{2,1,0:T(4,128)(2,1)} %reshape.80), calls=%async_computation.1 | async-start | bytes 1048576 | tf_op jit(solution)/shard_map/all_to_all | solution.py:80
  71.0 54.1 %all-gather.10.cloned.1.call-start = ((), (), s32[]{:S(2)}) async-start(), calls=%async_computation.2 | async-start | bytes 1114112 | tf_op jit(solution)/shard_map/all_gather | solution.py:108
  86.8 119.4 %copy-start.2 = (bf16[8,4096]{1,0:T(8,128)(2,1)}, bf16[8,4096]{1,0:T(8,128)(2,1)S(1)}, u32[]{:S(2)}) copy-start(bf16[8,4096]{1,0:T(8,128)(2,1)S(1)} %get-tuple-element.88) | copy-start | bytes 196612
Sparse Core Ops, SparseCore 0:
  87.7 37.3 all-gather.9
where the time goes:
time: 213 us
  blocking collectives  105 us (49%)
  matrix products  42.7 us (20%)
  waiting for transfers between devices  38.4 us (18%)
  between operations  14.9 us (7%)
  local copies, waits for them, and re-layouts  4.72 us (2%)
  starting transfers between devices  4.21 us (2%)
  other arithmetic  2.76 us (1%)
    all_gather x4, blocking collectives, joined(): pieces = jax.tree.map(lambda part: lax.all_gather(part, axis), value)  73 us
    all_gather x1, waiting for transfers between devices, on_device(): lax.all_gather(normed, 'expert', axis=0, tiled=True)  25 us
    dot_general x1, matrix products, on_device(): jnp.dot(act, w_down, preferred_element_type=jnp.float32)  21.8 us
    all_to_all x1, blocking collectives, on_device(): lax.all_to_all(outgoing, 'expert', split_axis=0, concat_axis=0, tiled=True)  21.5 us
    all_to_all x1, waiting for transfers between devices, on_device(): lax.all_to_all(partial_out.reshape(devices, slot_count, model_width), 'ex...  13.4 us
    dot_general x1, matrix products, on_device(): gate_act = jnp.dot(flat_rows, w_gate, preferred_element_type=jnp.float32)  11.9 us
    unnamed x1, blocking collectives  10.5 us
    dot_general x1, matrix products, on_device(): jnp.dot(lax.all_gather(normed, 'expert', axis=0, tiled=True), head_weight...  5.05 us
  transfers between devices with their start and end apart: 2, of which 2 were waited for; matrix products, arithmetic and copies ran while one was open for 1% of the time, Pallas kernels for 0%

commit v1 on v0

v1 whole, which is shorter than its diff:
```python
import functools
import jax
import jax.numpy as jnp
from jax import lax
from jax.experimental import pallas as pl
from jax.experimental.pallas import tpu as pltpu
from jax.sharding import PartitionSpec as P

EXPERTS = 8
DOM_DEV = 2
BINS = 16
CAP = 3
PAD = 4
F32 = jnp.float32
BF16 = jnp.bfloat16
HIGHEST = lax.Precision.HIGHEST


def iota(shape, dim):
    return lax.broadcasted_iota(jnp.int32, shape, dim)


def kernel(cfg, tokens, ids_row, meta, router_t, gain, w_gate, w_up, w_down, head,
           out_hidden, out_stats,
           gu_buf, dn_buf, hd_buf, send_d, recv_d, x_buf, act_buf, p_buf, r1_buf, s_buf, r2_buf,
           h_buf, meta_buf, st_send, st_buf, scores, ssq, wt_buf,
           gu_sem, dn_sem, hd_sem, own_sem, d1_send, d1_recv, d2_send, d2_recv, r1_send, r1_recv,
           r2_send, r2_recv, ag_send, ag_recv, mt_send, mt_recv, st_ssem, st_rsem):
    n, G, C, X, Z = cfg["n"], cfg["G"], cfg["C"], cfg["X"], cfg["Z"]
    rows, D = tokens.shape
    half = D // 2
    E = EXPERTS
    TF, NF, NGU = cfg["TF"], cfg["NF"], cfg["NGU"]
    TD, ND, NDW = cfg["TD"], cfg["ND"], cfg["NDW"]
    NCH = cfg["NCH"]
    Nc = D // NCH
    hc = Nc // 2
    per_chunk = ND // NCH
    me = lax.axis_index("expert")
    me_e, me_g = me // G, me % G
    mz, mx, mc = me // (C * X), (me // C) % X, me % C
    my_place = (mc * X + mx) * Z + mz

    def remote(src, dst, ss, rs, peer):
        return pltpu.make_async_remote_copy(
            src_ref=src, dst_ref=dst, send_sem=ss, recv_sem=rs,
            device_id={"expert": peer}, device_id_type=pl.DeviceIdType.MESH)

    def drain(ref, sem):
        pltpu.make_async_copy(ref, ref, sem).wait()

    def gu_copy(t, src, which, slot):
        return pltpu.make_async_copy(
            src.at[:, pl.ds(pl.multiple_of(t * TF, TF if TF % 128 == 0 else 1), TF)] if NF > 1 else src,
            gu_buf.at[slot, which], gu_sem.at[slot, which])

    def gu_start(t, slot):
        gu_copy(t, w_gate, 0, slot).start()
        gu_copy(t, w_up, 1, slot).start()

    def dn_copy(t, slot):
        return pltpu.make_async_copy(
            w_down.at[:, pl.ds(t * TD, TD)], dn_buf.at[slot], dn_sem.at[slot])

    def hd_copy(c):
        return pltpu.make_async_copy(head.at[pl.ds(c * Nc, Nc)], hd_buf.at[c], hd_sem.at[c])

    for t in range(NGU):
        gu_start(t, t)
    barrier = pltpu.get_barrier_semaphore()

    def greet(o, carry):
        pl.semaphore_signal(barrier, inc=1, device_id={"expert": (me + o) % n},
                            device_id_type=pl.DeviceIdType.MESH)
        return carry

    lax.fori_loop(1, n, greet, 0)
    for t in range(NDW):
        dn_copy(t, t).start()

    RB = E * 2 * PAD
    r = iota((RB, rows), 0)
    r_e, r_h, r_s = r // (2 * PAD), (r % (2 * PAD)) // PAD, r % PAD
    member = ((ids_row[0:1, :] == r_e) | (ids_row[1:2, :] == r_e)).astype(F32)
    upper = (iota((rows, rows), 0) < iota((rows, rows), 1)).astype(F32)
    slot = jnp.dot(member, upper, preferred_element_type=F32)
    lay = member * (slot == r_s.astype(F32)).astype(F32)
    lay_lo = (lay * (r_h == 0).astype(F32)).astype(BF16)
    lay_hi = (lay * (r_h == 1).astype(F32)).astype(BF16)
    packed = (jnp.dot(lay_lo, tokens[:, :half], preferred_element_type=F32)
              + jnp.dot(lay_hi, tokens[:, half:], preferred_element_type=F32))
    send_d[...] = packed.reshape(E, 2 * PAD, half).astype(BF16)
    meta_buf[my_place] = meta[...]

    pl.semaphore_wait(barrier, n - 1)

    d1 = []
    for o in range(1, E):
        e = (me_e + o) % E
        cp = remote(send_d.at[e], recv_d.at[me_g, me_e], d1_send.at[o], d1_recv.at[o], e * G + me_g)
        cp.start()
        d1.append(cp)
    own = pltpu.make_async_copy(send_d.at[me_e], recv_d.at[me_g, me_e], own_sem)
    own.start()

    def meta_send(o, carry):
        remote(meta, meta_buf.at[my_place], mt_send, mt_recv, (me + o) % n).start()
        return carry

    tok32 = tokens[...].astype(F32)
    ids0, ids1 = meta[:, 0:1], meta[:, 1:2]
    c0 = jnp.zeros((rows, 1), F32)
    c1 = jnp.zeros((rows, 1), F32)
    for e in range(E):
        logit = jnp.sum(tok32 * router_t[e:e + 1, :], axis=1, keepdims=True)
        c0 = c0 + jnp.where(ids0 == e, logit, 0.0)
        c1 = c1 + jnp.where(ids1 == e, logit, 0.0)
    g0 = 1.0 / (1.0 + jnp.exp(c1 - c0))
    g1 = 1.0 / (1.0 + jnp.exp(c0 - c1))
    q = iota((rows, RB), 1)
    q_e, q_h, q_s = q // (2 * PAD), (q % (2 * PAD)) // PAD, q % PAD
    is0, is1 = ids0 == q_e, ids1 == q_e
    member_t = (is0 | is1).astype(F32)
    lower = (iota((rows, rows), 1) < iota((rows, rows), 0)).astype(F32)
    slot_t = jnp.dot(lower, member_t, preferred_element_type=F32)
    weight = (jnp.where(is0, g0, 0.0) + jnp.where(is1, g1, 0.0)) * (
        slot_t == q_s.astype(F32)).astype(F32)
    wt_buf[0] = weight * (q_h == 0).astype(F32)
    wt_buf[1] = weight * (q_h == 1).astype(F32)

    own.wait()
    d2 = []
    for o in range(E):
        e = (me_e - o + E) % E
        if o > 0:
            d1[o - 1].wait_recv()
        for k in range(1, G):
            cp = remote(recv_d.at[me_g, e], recv_d.at[me_g, e], d2_send.at[k], d2_recv.at[k],
                        me_e * G + (me_g + k) % G)
            cp.start()
    for k in range(1, G):
        drain(recv_d.at[(me_g - k + G) % G], d2_recv.at[k])

    M = n * PAD
    pick_r, pick_c = iota((M, n * 2 * PAD), 0), iota((M, n * 2 * PAD), 1)
    base = (pick_r // PAD) * (2 * PAD) + pick_r % PAD
    sel_lo = (pick_c == base).astype(BF16)
    sel_hi = (pick_c == base + PAD).astype(BF16)
    W = 512
    for j in range(half // W):
        got = recv_d[:, :, :, j * W:(j + 1) * W].astype(F32).reshape(n * 2 * PAD, W).astype(BF16)
        x_buf[:, j * W:(j + 1) * W] = jnp.dot(
            sel_lo, got, preferred_element_type=F32).astype(BF16)
        x_buf[:, half + j * W:half + (j + 1) * W] = jnp.dot(
            sel_hi, got, preferred_element_type=F32).astype(BF16)

    lax.fori_loop(1, n, meta_send, 0)

    def expert_tile(t, carry):
        s = t % NGU
        gu_copy(t, w_gate, 0, s).wait()
        g = jnp.dot(x_buf[...], gu_buf[s, 0], preferred_element_type=F32)
        gu_copy(t, w_up, 1, s).wait()
        u = jnp.dot(x_buf[...], gu_buf[s, 1], preferred_element_type=F32)
        a = (g / (1.0 + jnp.exp(-g)) * u).astype(BF16)
        act_buf[t] = a

        @pl.when(t + NGU < NF)
        def _():
            gu_start(t + NGU, s)

        return carry

    lax.fori_loop(0, NF, expert_tile, 0)
    for c in range(NCH):
        hd_copy(c).start()

    br = iota((RB, E * PAD), 0)
    bc = iota((RB, E * PAD), 1)
    b_src = (br // (2 * PAD)) * PAD + br % PAD
    b_h = (br % (2 * PAD)) // PAD
    blk_lo = ((bc == b_src) & (b_h == 0)).astype(BF16)
    blk_hi = ((bc == b_src) & (b_h == 1)).astype(BF16)

    def down(c):
        for i in range(per_chunk):
            t = c * per_chunk + i
            s = t % NDW
            dn_copy(t, s).wait()
            acc = jnp.dot(act_buf[0], dn_buf[s, 0:TF], preferred_element_type=F32)
            for f in range(1, NF):
                acc = acc + jnp.dot(act_buf[f], dn_buf[s, f * TF:(f + 1) * TF],
                                    preferred_element_type=F32)
            p_buf[c, :, :, i * TD:(i + 1) * TD] = acc.astype(BF16).reshape(G, E * PAD, TD)
            if t + NDW < ND:
                dn_copy(t + NDW, s).start()
        for k in range(1, G):
            remote(p_buf.at[c, (me_g + k) % G], r1_buf.at[c, k], r1_send.at[c, k], r1_recv.at[c, k],
                   me_e * G + (me_g + k) % G).start()

    def stage2(c):
        total = p_buf[c, me_g].astype(F32)
        for k in range(1, G):
            drain(r1_buf.at[c, k], r1_recv.at[c, k])
            total = total + r1_buf[c, k].astype(F32)
        summed = total.astype(BF16)
        block = (jnp.dot(blk_lo, summed[:, :hc], preferred_element_type=F32)
                 + jnp.dot(blk_hi, summed[:, hc:], preferred_element_type=F32))
        s_buf[c] = block.reshape(E, 2 * PAD, hc).astype(BF16)
        r2_buf[c, me_e] = s_buf[c, me_e]
        for o in range(1, E):
            e = (me_e + o) % E
            remote(s_buf.at[c, e], r2_buf.at[c, me_e], r2_send.at[c], r2_recv.at[c],
                   e * G + me_g).start()

    def stage3(c):
        drain(r2_buf.at[c, pl.ds(0, E - 1)], r2_recv.at[c])
        got = r2_buf[c].astype(F32).reshape(RB, hc)
        at = c * Nc
        for h in range(2):
            moe = jnp.dot(wt_buf[h], got, precision=HIGHEST, preferred_element_type=F32)
            lo = at + h * hc
            hid = (tokens[:, lo:lo + hc].astype(F32) + moe).astype(BF16)
            out_hidden[:, lo:lo + hc] = hid
            h_buf[c, mc, mx, mz, :, h * hc:(h + 1) * hc] = hid
        src = h_buf.at[c, mc, mx, mz]
        for o in range(1, Z):
            remote(src, src, ag_send.at[c, 0], ag_recv.at[c, 0],
                   (((mz + o) % Z) * X + mx) * C + mc).start()

    def gather2(c):
        drain(h_buf.at[c, mc, mx, pl.ds(0, Z - 1)], ag_recv.at[c, 0])
        src = h_buf.at[c, mc, mx]
        for o in range(1, X):
            remote(src, src, ag_send.at[c, 1], ag_recv.at[c, 1],
                   (mz * X + (mx + o) % X) * C + mc).start()

    def gather3(c):
        drain(h_buf.at[c, mc, pl.ds(0, X - 1)], ag_recv.at[c, 1])
        src = h_buf.at[c, mc]
        for o in range(1, C):
            remote(src, src, ag_send.at[c, 2], ag_recv.at[c, 2],
                   (mz * X + mx) * C + (mc + o) % C).start()

    def head_part(c):
        drain(h_buf.at[c, pl.ds(0, C - 1)], ag_recv.at[c, 2])
        wide = h_buf[c].astype(F32).reshape(n * rows, Nc)
        sq = jnp.sum(wide * wide, axis=1, keepdims=True)
        scaled = (wide * gain[:, c * Nc:(c + 1) * Nc]).astype(BF16)
        hd_copy(c).wait()
        part = jnp.dot(scaled, hd_buf[c], preferred_element_type=F32)
        if c == 0:
            scores[...] = part
            ssq[...] = sq
        else:
            scores[...] += part
            ssq[...] += sq

    stages = [(down, 0.0), (stage2, 2.1), (stage3, 6.1), (gather2, 9.1), (gather3, 11.1), (head_part, 13.1)]
    plan = []
    for c in range(NCH):
        for at, (fn, when) in enumerate(stages):
            plan.append((2.0 * c + when, at, c, fn))
    for _, _, c, fn in sorted(plan, key=lambda item: item[:3]):
        fn(c)

    drain(meta_buf.at[pl.ds(0, n - 1)], mt_recv)
    R = n * rows
    V = scores.shape[1]
    sc = scores[...] * lax.rsqrt(ssq[...] * (1.0 / D) + 1.0)
    ids = meta_buf[...].reshape(R, 128)
    top = jnp.max(sc, axis=1, keepdims=True)
    ex = jnp.exp(sc - top)
    mass = jnp.sum(ex, axis=1, keepdims=True)
    moment = jnp.sum(ex * sc, axis=1, keepdims=True)
    column = iota((R, V), 1) + me * V
    hit = jnp.sum(jnp.where(ids[:, 2:3] == column, sc, 0.0), axis=1, keepdims=True)
    lane = iota((R, 128), 1)
    stat = jnp.where(lane == 0, top, jnp.where(lane == 1, mass, jnp.where(
        lane == 2, moment, jnp.where(lane == 3, hit, 0.0))))
    turned = stat.T[0:8, :]
    st_send[...] = turned
    st_buf[me] = turned

    def stat_send(o, carry):
        remote(st_send, st_buf.at[me], st_ssem, st_rsem, (me + o) % n).start()
        return carry

    lax.fori_loop(1, n, stat_send, 0)

    dom, bins = ids[:, 3:4], ids[:, 4:5]
    col = iota((R, 128), 1)
    spot = (dom - me * DOM_DEV) * BINS + bins
    inside = (dom >= me * DOM_DEV) & (dom < (me + 1) * DOM_DEV)
    own_row = my_place * rows
    hot = ((inside & (col == spot)) | (
        (col >= 64) & (col < 64 + rows) & (iota((R, 128), 0) == own_row + col - 64))).astype(F32)

    for cp in d1:
        cp.wait_send()
    for k in range(1, G):
        drain(recv_d.at[me_g], d2_send.at[k])
    for c in range(NCH):
        for k in range(1, G):
            drain(r1_buf.at[c, k], r1_send.at[c, k])
        drain(r2_buf.at[c, pl.ds(0, E - 1)], r2_send.at[c])
        drain(h_buf.at[c, mc, mx, pl.ds(0, Z - 1)], ag_send.at[c, 0])
        drain(h_buf.at[c, mc, pl.ds(0, X - 1)], ag_send.at[c, 1])
        drain(h_buf.at[c, pl.ds(0, C - 1)], ag_send.at[c, 2])
    drain(meta_buf.at[pl.ds(0, n - 1)], mt_send)
    drain(st_buf.at[pl.ds(0, n - 1)], st_ssem)
    drain(st_buf.at[pl.ds(0, n - 1)], st_rsem)
    tops = st_buf[:, 0, :]
    joined = jnp.max(tops, axis=0, keepdims=True)
    factor = jnp.exp(tops - joined)
    mass_all = jnp.sum(st_buf[:, 1, :] * factor, axis=0, keepdims=True)
    moment_all = jnp.sum(st_buf[:, 2, :] * factor, axis=0, keepdims=True)
    target = jnp.sum(st_buf[:, 3, :], axis=0, keepdims=True)
    log_norm = joined + jnp.log(mass_all)
    nll = log_norm - target
    ent = log_norm - moment_all / mass_all
    kind = iota((8, R), 0)
    vals = jnp.where(kind == 0, 1.0, jnp.where(kind == 1, nll, jnp.where(kind == 2, ent, 0.0)))
    out_stats[...] = jnp.dot(vals, hot, precision=HIGHEST, preferred_element_type=F32)


def on_device(tokens, router, w_gate, w_up, w_down, norm_gain, head_weight, expert_ids, targets,
              domains, bins):
    n = lax.axis_size("expert")
    rows, D = tokens.shape
    F = w_down.shape[0]
    V = head_weight.shape[1]
    G = n // EXPERTS
    C, X = 2, 2
    Z = n // (C * X)
    TF = 512 if F % 512 == 0 else F
    NF = F // TF
    TD = 512
    ND = D // TD
    NCH = 4
    cfg = dict(n=n, G=G, C=C, X=X, Z=Z, TF=TF, NF=NF, NGU=min(3, NF), TD=TD, ND=ND,
               NDW=min(5, ND), NCH=NCH)
    Nc = D // NCH
    hc = Nc // 2
    lane = jnp.arange(128, dtype=jnp.int32)[None, :]
    meta = jnp.where(lane == 0, expert_ids[:, 0:1], jnp.where(
        lane == 1, expert_ids[:, 1:2], jnp.where(
            lane == 2, targets[:, None], jnp.where(
                lane == 3, domains[:, None], jnp.where(lane == 4, bins[:, None], 0)))))
    vmem = pl.BlockSpec(memory_space=pltpu.VMEM)
    hbm = pl.BlockSpec(memory_space=pltpu.HBM)
    DMA = pltpu.SemaphoreType.DMA
    M = n * PAD
    scratch = [
        pltpu.VMEM((cfg["NGU"], 2, D, TF), BF16),
        pltpu.VMEM((cfg["NDW"], F, TD), BF16),
        pltpu.VMEM((NCH, Nc, V), BF16),
        pltpu.VMEM((EXPERTS, 2 * PAD, D // 2), BF16),
        pltpu.VMEM((G, EXPERTS, 2 * PAD, D // 2), BF16),
        pltpu.VMEM((M, D), BF16),
        pltpu.VMEM((NF, M, TF), BF16),
        pltpu.VMEM((NCH, G, EXPERTS * PAD, Nc), BF16),
        pltpu.VMEM((NCH, G, EXPERTS * PAD, Nc), BF16),
        pltpu.VMEM((NCH, EXPERTS, 2 * PAD, hc), BF16),
        pltpu.VMEM((NCH, EXPERTS, 2 * PAD, hc), BF16),
        pltpu.VMEM((NCH, C, X, Z, rows, Nc), BF16),
        pltpu.VMEM((n, rows, 128), jnp.int32),
        pltpu.VMEM((8, n * rows), F32),
        pltpu.VMEM((n, 8, n * rows), F32),
        pltpu.VMEM((n * rows, V), F32),
        pltpu.VMEM((n * rows, 1), F32),
        pltpu.VMEM((2, rows, EXPERTS * 2 * PAD), F32),
        DMA((cfg["NGU"], 2)), DMA((cfg["NDW"],)), DMA((NCH,)), DMA(()),
        DMA((EXPERTS,)), DMA((EXPERTS,)), DMA((G,)), DMA((G,)),
        DMA((NCH, G)), DMA((NCH, G)), DMA((NCH,)), DMA((NCH,)),
        DMA((NCH, 3)), DMA((NCH, 3)), DMA(()), DMA(()), DMA(()), DMA(()),
    ]
    hidden, stats = pl.pallas_call(
        functools.partial(kernel, cfg),
        out_shape=(jax.ShapeDtypeStruct((rows, D), BF16), jax.ShapeDtypeStruct((8, 128), F32)),
        in_specs=[vmem] * 5 + [hbm] * 4,
        out_specs=(vmem, vmem),
        scratch_shapes=scratch,
        compiler_params=pltpu.CompilerParams(
            collective_id=0, has_side_effects=True, vmem_limit_bytes=67043328),
    )(tokens, expert_ids.T, meta, router.T, norm_gain[None, :], w_gate, w_up, w_down, head_weight)
    token_nll = stats[1, 64:64 + rows]
    domain_table = stats[0:3, 0:DOM_DEV * BINS].reshape(3, DOM_DEV, BINS)
    return hidden, token_nll, domain_table


def solution(mesh):
    return jax.shard_map(
        on_device,
        mesh=mesh,
        in_specs=(
            P(("groups", "expert"), None),
            P(),
            P(None, "expert"),
            P(None, "expert"),
            P("expert", None),
            P(),
            P(None, "expert"),
            P(("groups", "expert"), None),
            P(("groups", "expert")),
            P(("groups", "expert")),
            P(("groups", "expert")),
        ),
        out_specs=(
            P(("groups", "expert"), None),
            P(("groups", "expert")),
            P(None, ("groups", "expert"), None),
        ),
        check_vma=False,
    )
```

time: 213 us -> 67.3 us (0.32)
  blocking collectives: 105 us -> 0 us
  Pallas kernels: 0 us -> 60.2 us
  matrix products: 42.7 us -> 0 us
  waiting for transfers between devices: 38.4 us -> 0 us
  between operations: 14.9 us -> 0.65 us
  starting transfers between devices: 4.21 us -> 0 us
    all_gather x4 -> x0, blocking collectives: 73 us -> none  [joined(): pieces = jax.tree.map(lambda part: lax.all_gather(part, axis), value)]
    pallas_call x0 -> x1, Pallas kernels: none -> 60.2 us  [on_device(): pl.pallas_call(functools.partial(kernel, cfg), out_shape=(jax.ShapeDtypeS...]
    dot_general x9 -> x0, matrix products: 42.7 us -> none  [the longest x1 21.8 us: on_device(): jnp.dot(act, w_down, preferred_element_type=jnp.float32)]
    all_gather x1 -> x0, waiting for transfers between devices: 25 us -> none  [on_device(): lax.all_gather(normed, 'expert', axis=0, tiled=True)]
    all_to_all x1 -> x0, blocking collectives: 21.5 us -> none  [on_device(): lax.all_to_all(outgoing, 'expert', split_axis=0, concat_axis=0, tiled=True)]
    all_to_all x1 -> x0, waiting for transfers between devices: 13.4 us -> none  [on_device(): lax.all_to_all(partial_out.reshape(devices, slot_count, model_width), 'ex...]
    unnamed x1 -> x0, blocking collectives: 10.5 us -> none
    all_to_all x1 -> x0, starting transfers between devices: 4.17 us -> none  [on_device(): lax.all_to_all(partial_out.reshape(devices, slot_count, model_width), 'ex...]
  transfers between devices with their start and end apart: 2 -> 0, of which waited for: 2 -> 0; matrix products, arithmetic and copies ran while one was open for 1% -> 0% of each run, Pallas kernels for 0% -> 0%
where the time goes in v1:
time: 67.3 us; the launch traced here: 67.1 us
  Pallas kernels  60.2 us (89%)
  local copies, waits for them, and re-layouts  4.82 us (7%)
  other arithmetic  1.37 us (2%)
    pallas_call x1, Pallas kernels, on_device(): pl.pallas_call(functools.partial(kernel, cfg), out_shape=(jax.ShapeDtypeS...  60.2 us
    unnamed x1, local copies, waits for them, and re-layouts  1.47 us
    select_n x1, other arithmetic, on_device(): jnp.where(lane == 0, expert_ids[:, 0:1], jnp.where(lane == 1, expert_ids[...  1.35 us

profile of v1, /device:TPU:0, one launch (start us, length us, event | category | flops | bytes accessed | tf_op | source)
XLA Modules:
  0.0 67.1 jit_solution(2358609021649423127)
XLA Ops:
  0.7 0.8 %slice_bitcast_fusion.2 = (s32[8]{0:T(128)S(1)}, s32[8]{0:T(128)S(1)}) fusion(s32[8,2]{0,1:T(2,128)} %param.18), kind=kLoop, calls=%fused_computation.7 | loop fusion | bytes 128 | tf_op jit(solution)/shard_map/jit(_where)/broadcast_in_dim | solution.py:346
  1.4 1.4 %select_select_fusion.meta = s32[8,128]{1,0:T(8,128)} fusion(s32[8]{0:T(128)} %param.21, s32[8]{0:T(128)} %param.20, s32[8]{0:T(128)} %param.19, s32[8]{0:T(128)S(1)} %get-tuple-element.8, s32[8]{0:T(128)S(1)} %get-tuple-element.7, pred[128]{0:T(512)(128)(4,1)S(1)} %get-tuple-element.9, pred[128]{0:T(512)(128)(4,1)S(1)} %get-tuple-element.10, ...), kind=kLoop, calls=%fused_computation | loop fusion | flops 5120 | bytes 4896 | tf_op jit(solution)/shard_map/jit(_where)/select_n | solution.py:346
  2.8 60.2 %shard_map.130 = (bf16[8,4096]{1,0:T(8,128)(2,1)}, f32[8,128]{1,0:T(8,128)}) custom-call(bf16[8,4096]{1,0:T(8,128)(2,1)} %tokens.1, s32[2,8]{1,0:T(2,128)} %bitcast.11, s32[8,128]{1,0:T(8,128)} %select_select_fusion.meta, f32[8,4096]{1,0:T(8,128)} %bitcast.9, f32[1,4096]{1,0:T(1,128)} %bitcast.10, bf16[4096,3584]{1,0:T(8,128)(2,1)} %w_gate.1, ...), custom_call_target="tpu_custom_call" | custom-call | tf_op jit(solution)/shard_map/pallas_call | solution.py:378
  63.0 0.7 %slice.15 = f32[3,32]{1,0:T(4,128)S(1)} slice(f32[8,128]{1,0:T(8,128)} %get-tuple-element.6), slice={[0:3], [0:32]} | slice | bytes 768 | tf_op jit(solution)/shard_map/slice | solution.py:388
  63.7 0.7 reshape.37
  64.3 1.3 %slice_bitcast_fusion = f32[8]{0:T(128)} fusion(f32[8,128]{1,0:T(8,128)} %get-tuple-element.6), kind=kLoop, calls=%fused_computation.1 | loop fusion | bytes 64 | tf_op jit(solution)/shard_map/squeeze | solution.py:387
  65.6 1.5 %copy.15 = bf16[8,4096]{1,0:T(8,128)(2,1)} copy(bf16[8,4096]{1,0:T(8,128)(2,1)} %get-tuple-element.16) | data formatting | bytes 131072
  (3 shorter events, 0.0 us)

commit v2 on v1

--- a/solution.py
+++ b/solution.py
@@ -20,8 +20,8 @@
     return lax.broadcasted_iota(jnp.int32, shape, dim)
 
 
-def kernel(cfg, tokens, ids_row, meta, router_t, gain, w_gate, w_up, w_down, head,
-           out_hidden, out_stats,
+def kernel(cfg, tokens, ids_row, tgt_row, dom_row, bin_row, router_t, gain, w_gate, w_up, w_down,
+           head, out_hidden, out_nll, out_table,
            gu_buf, dn_buf, hd_buf, send_d, recv_d, x_buf, act_buf, p_buf, r1_buf, s_buf, r2_buf,
            h_buf, meta_buf, st_send, st_buf, scores, ssq, wt_buf,
            gu_sem, dn_sem, hd_sem, own_sem, d1_send, d1_recv, d2_send, d2_recv, r1_send, r1_recv,
@@ -90,7 +90,16 @@
     packed = (jnp.dot(lay_lo, tokens[:, :half], preferred_element_type=F32)
               + jnp.dot(lay_hi, tokens[:, half:], preferred_element_type=F32))
     send_d[...] = packed.reshape(E, 2 * PAD, half).astype(BF16)
-    meta_buf[my_place] = meta[...]
+    eye = iota((rows, rows), 0) == iota((rows, rows), 1)
+
+    def column_of(row):
+        wide = jnp.where(eye, row.astype(F32), 0.0)
+        return jnp.sum(wide, axis=1, keepdims=True).astype(jnp.int32)
+
+    ids0, ids1 = column_of(ids_row[0:1, :]), column_of(ids_row[1:2, :])
+    ml = iota((rows, 128), 1)
+    meta_buf[my_place] = jnp.where(ml == 2, column_of(tgt_row[...]), jnp.where(
+        ml == 3, column_of(dom_row[...]), jnp.where(ml == 4, column_of(bin_row[...]), 0)))
 
     pl.semaphore_wait(barrier, n - 1)
 
@@ -104,11 +113,10 @@
     own.start()
 
     def meta_send(o, carry):
-        remote(meta, meta_buf.at[my_place], mt_send, mt_recv, (me + o) % n).start()
+        remote(meta_buf.at[my_place], meta_buf.at[my_place], mt_send, mt_recv, (me + o) % n).start()
         return carry
 
     tok32 = tokens[...].astype(F32)
-    ids0, ids1 = meta[:, 0:1], meta[:, 1:2]
     c0 = jnp.zeros((rows, 1), F32)
     c1 = jnp.zeros((rows, 1), F32)
     for e in range(E):
@@ -172,8 +180,6 @@
         return carry
 
     lax.fori_loop(0, NF, expert_tile, 0)
-    for c in range(NCH):
-        hd_copy(c).start()
 
     br = iota((RB, E * PAD), 0)
     bc = iota((RB, E * PAD), 1)
@@ -194,6 +200,9 @@
             p_buf[c, :, :, i * TD:(i + 1) * TD] = acc.astype(BF16).reshape(G, E * PAD, TD)
             if t + NDW < ND:
                 dn_copy(t + NDW, s).start()
+            if t + 1 == max(ND - NDW, 1):
+                for h in range(NCH):
+                    hd_copy(h).start()
         for k in range(1, G):
             remote(p_buf.at[c, (me_g + k) % G], r1_buf.at[c, k], r1_send.at[c, k], r1_recv.at[c, k],
                    me_e * G + (me_g + k) % G).start()
@@ -321,7 +330,10 @@
     ent = log_norm - moment_all / mass_all
     kind = iota((8, R), 0)
     vals = jnp.where(kind == 0, 1.0, jnp.where(kind == 1, nll, jnp.where(kind == 2, ent, 0.0)))
-    out_stats[...] = jnp.dot(vals, hot, precision=HIGHEST, preferred_element_type=F32)
+    res = jnp.dot(vals, hot, precision=HIGHEST, preferred_element_type=F32)
+    out_nll[...] = res[1:2, 64:64 + rows]
+    for d in range(DOM_DEV):
+        out_table[:, d, :] = res[0:3, d * BINS:(d + 1) * BINS]
 
 
 def on_device(tokens, router, w_gate, w_up, w_down, norm_gain, head_weight, expert_ids, targets,
@@ -339,14 +351,9 @@
     ND = D // TD
     NCH = 4
     cfg = dict(n=n, G=G, C=C, X=X, Z=Z, TF=TF, NF=NF, NGU=min(3, NF), TD=TD, ND=ND,
-               NDW=min(5, ND), NCH=NCH)
+               NDW=min(6, ND), NCH=NCH)
     Nc = D // NCH
     hc = Nc // 2
-    lane = jnp.arange(128, dtype=jnp.int32)[None, :]
-    meta = jnp.where(lane == 0, expert_ids[:, 0:1], jnp.where(
-        lane == 1, expert_ids[:, 1:2], jnp.where(
-            lane == 2, targets[:, None], jnp.where(
-                lane == 3, domains[:, None], jnp.where(lane == 4, bins[:, None], 0)))))
     vmem = pl.BlockSpec(memory_space=pltpu.VMEM)
     hbm = pl.BlockSpec(memory_space=pltpu.HBM)
     DMA = pltpu.SemaphoreType.DMA
@@ -375,18 +382,18 @@
         DMA((NCH, G)), DMA((NCH, G)), DMA((NCH,)), DMA((NCH,)),
         DMA((NCH, 3)), DMA((NCH, 3)), DMA(()), DMA(()), DMA(()), DMA(()),
     ]
-    hidden, stats = pl.pallas_call(
+    hidden, nll, table = pl.pallas_call(
         functools.partial(kernel, cfg),
-        out_shape=(jax.ShapeDtypeStruct((rows, D), BF16), jax.ShapeDtypeStruct((8, 128), F32)),
-        in_specs=[vmem] * 5 + [hbm] * 4,
-        out_specs=(vmem, vmem),
+        out_shape=(jax.ShapeDtypeStruct((rows, D), BF16), jax.ShapeDtypeStruct((1, rows), F32),
+                   jax.ShapeDtypeStruct((3, DOM_DEV, BINS), F32)),
+        in_specs=[vmem] * 7 + [hbm] * 4,
+        out_specs=(vmem, vmem, vmem),
         scratch_shapes=scratch,
         compiler_params=pltpu.CompilerParams(
             collective_id=0, has_side_effects=True, vmem_limit_bytes=67043328),
-    )(tokens, expert_ids.T, meta, router.T, norm_gain[None, :], w_gate, w_up, w_down, head_weight)
-    token_nll = stats[1, 64:64 + rows]
-    domain_table = stats[0:3, 0:DOM_DEV * BINS].reshape(3, DOM_DEV, BINS)
-    return hidden, token_nll, domain_table
+    )(tokens, expert_ids.T, targets[None, :], domains[None, :], bins[None, :], router.T,
+      norm_gain[None, :], w_gate, w_up, w_down, head_weight)
+    return hidden, nll[0], table
 
 
 def solution(mesh):

time: 67.3 us -> 65.1 us (0.967)
  other arithmetic: 1.37 us -> 0 us
  local copies, waits for them, and re-layouts: 4.82 us -> 3.84 us
    unnamed x1 -> x3, local copies, waits for them, and re-layouts: 1.47 us -> 3.84 us
    select_n x1 -> x0, other arithmetic: 1.35 us -> none  [on_device(): jnp.where(lane == 0, expert_ids[:, 0:1], jnp.where(lane == 1, expert_ids[...]
    squeeze x1 -> x0, local copies, waits for them, and re-layouts: 1.25 us -> none  [on_device(): token_nll = stats[1, 64:64 + rows]]
    broadcast_in_dim x1 -> x0, local copies, waits for them, and re-layouts: 0.76 us -> none  [on_device(): jnp.where(lane == 0, expert_ids[:, 0:1], jnp.where(lane == 1, expert_ids[...]
    slice x1 -> x0, local copies, waits for them, and re-layouts: 0.67 us -> none  [on_device(): domain_table = stats[0:3, 0:DOM_DEV * BINS].reshape(3, DOM_DEV, BINS)]
where the time goes in v2:
time: 65.1 us; the launch traced here: 64.8 us
  Pallas kernels  60.4 us (93%)
  local copies, waits for them, and re-layouts  3.84 us (6%)
    pallas_call x1, Pallas kernels, on_device(): pl.pallas_call(functools.partial(kernel, cfg), out_shape=(jax.ShapeDtypeS...  60.4 us
    unnamed x3, local copies, waits for them, and re-layouts  3.84 us

profile of v2, /device:TPU:0, one launch (start us, length us, event | category | flops | bytes accessed | tf_op | source)
XLA Modules:
  0.0 64.8 jit_solution(2432992597507936850)
XLA Ops:
  0.6 60.4 %shard_map.130 = (bf16[8,4096]{1,0:T(8,128)(2,1)}, f32[1,8]{1,0:T(1,128)}, f32[3,2,16]{2,1,0:T(2,128)}) custom-call(bf16[8,4096]{1,0:T(8,128)(2,1)} %tokens.1, s32[2,8]{1,0:T(2,128)} %bitcast.9, s32[1,8]{1,0:T(1,128)} %bitcast.10, s32[1,8]{1,0:T(1,128)} %bitcast.11, s32[1,8]{1,0:T(1,128)} %bitcast.12, f32[8,4096]{1,0:T(8,128)} %bitcast.7, ...), custom_call_target="tpu_custom_call" | custom-call | tf_op jit(solution)/shard_map/pallas_call | solution.py:385
  61.0 1.5 %copy.17 = bf16[8,4096]{1,0:T(8,128)(2,1)} copy(bf16[8,4096]{1,0:T(8,128)(2,1)} %get-tuple-element.12) | data formatting | bytes 131072
  62.5 1.1 %copy.18 = f32[8]{0:T(128)} copy(f32[8]{0:T(128)} %bitcast.13) | data formatting | bytes 64
  63.6 1.3 %copy.19 = f32[3,2,16]{2,1,0:T(2,128)} copy(f32[3,2,16]{2,1,0:T(2,128)} %get-tuple-element.14) | data formatting | bytes 768

commit v3 on v2

--- a/solution.py
+++ b/solution.py
@@ -265,7 +265,7 @@
             scores[...] += part
             ssq[...] += sq
 
-    stages = [(down, 0.0), (stage2, 2.1), (stage3, 6.1), (gather2, 9.1), (gather3, 11.1), (head_part, 13.1)]
+    stages = [(down, 0.0), (stage2, 2.1), (stage3, 8.2), (gather2, 11.1), (gather3, 13.1), (head_part, 15.1)]
     plan = []
     for c in range(NCH):
         for at, (fn, when) in enumerate(stages):

time: 65.1 us -> 67.1 us (1.031)
  Pallas kernels: 60.4 us -> 62.4 us
    pallas_call x1, Pallas kernels: 60.4 us -> 62.4 us  [on_device(): pl.pallas_call(functools.partial(kernel, cfg), out_shape=(jax.ShapeDtypeS...]
where the time goes in v3:
time: 67.1 us; the launch traced here: 66.9 us
  Pallas kernels  62.4 us (93%)
  local copies, waits for them, and re-layouts  3.84 us (6%)
    pallas_call x1, Pallas kernels, on_device(): pl.pallas_call(functools.partial(kernel, cfg), out_shape=(jax.ShapeDtypeS...  62.4 us
    unnamed x3, local copies, waits for them, and re-layouts  3.84 us

profile of v3, /device:TPU:0, one launch (start us, length us, event | category | flops | bytes accessed | tf_op | source)
XLA Modules:
  0.0 66.9 jit_solution(3478443249568905675)
XLA Ops:
  0.6 62.4 %shard_map.130 = (bf16[8,4096]{1,0:T(8,128)(2,1)}, f32[1,8]{1,0:T(1,128)}, f32[3,2,16]{2,1,0:T(2,128)}) custom-call(bf16[8,4096]{1,0:T(8,128)(2,1)} %tokens.1, s32[2,8]{1,0:T(2,128)} %bitcast.9, s32[1,8]{1,0:T(1,128)} %bitcast.10, s32[1,8]{1,0:T(1,128)} %bitcast.11, s32[1,8]{1,0:T(1,128)} %bitcast.12, f32[8,4096]{1,0:T(8,128)} %bitcast.7, ...), custom_call_target="tpu_custom_call" | custom-call | tf_op jit(solution)/shard_map/pallas_call | solution.py:385
  63.0 1.5 %copy.17 = bf16[8,4096]{1,0:T(8,128)(2,1)} copy(bf16[8,4096]{1,0:T(8,128)(2,1)} %get-tuple-element.12) | data formatting | bytes 131072
  64.5 1.1 %copy.18 = f32[8]{0:T(128)} copy(f32[8]{0:T(128)} %bitcast.13) | data formatting | bytes 64
  65.6 1.3 %copy.19 = f32[3,2,16]{2,1,0:T(2,128)} copy(f32[3,2,16]{2,1,0:T(2,128)} %get-tuple-element.14) | data formatting | bytes 768
